TPU v7x, 32 devices: a whole 2x2x4 slice. The times are simulated.
32 devices in a mesh: cuts: 4 (over z), fsdp: 8 (over y, x, core).
Axes of the slice: x: 2, y: 2, z: 4, core: 2. Of those that a mesh axis runs over, the one named last changes fastest.
Arguments:
- tokens: bfloat16 [4096, 8192], P(('cuts', 'fsdp')), may hold values from -240 to 240
- norm_gain: bfloat16 [8192], P('fsdp'), may hold values from 0.5 to 1.5
- gate_weight: bfloat16 [8192, 256], P('fsdp'), may hold values from -0.0625 to 0.0625
- up_weight: bfloat16 [8192, 256], P('fsdp'), may hold values from -0.0625 to 0.0625
- down_weight: bfloat16 [256, 8192], P(None, 'fsdp'), may hold values from -0.375 to 0.375
- slice_grads: float32 [4, 3, 8192, 256], P('cuts', None, 'fsdp'), may hold values from -6 to 6
Outputs:
- branch_out: bfloat16 [4096, 8192], P(('cuts', 'fsdp'))
- grad_mean: float32 [3, 8192, 256], P(None, 'fsdp')
All inputs are finite; a program needn't handle non-finite values.
Results may differ from a plain program's by a relative error of at most 0.0065.
Values may be sent and summed in bfloat16 or wider, within the bound.
A program may use at most 64 MiB of HBM per device.

v0:
```python
import jax
import jax.numpy as jnp
from jax import lax
from jax.sharding import PartitionSpec as P


def average_grads(slice_grads):
    summed = lax.psum(slice_grads[0], "cuts")
    return summed / lax.axis_size("cuts")


def per_device(tokens, norm_gain, gate_weight, up_weight, down_weight, slice_grads):
    tok_float = tokens.astype(jnp.float32)
    inv_rms = lax.rsqrt(jnp.mean(tok_float * tok_float, axis=1, keepdims=True) + 1e-05)
    gathered = (
        lax.all_gather(gate_weight, "fsdp", axis=0, tiled=True),
        lax.all_gather(up_weight, "fsdp", axis=0, tiled=True),
        lax.all_gather(norm_gain, "fsdp", axis=0, tiled=True),
    )
    normed = (tok_float * inv_rms * gathered[2].astype(jnp.float32)[None, :]).astype(jnp.bfloat16)
    gate_out = jnp.dot(normed, gathered[0], preferred_element_type=jnp.float32)
    up_out = jnp.dot(normed, gathered[1], preferred_element_type=jnp.float32)
    hidden = (jax.nn.silu(gate_out) * up_out).astype(jnp.bfloat16)
    down_full = lax.all_gather(down_weight, "fsdp", axis=1, tiled=True)
    branch = jnp.dot(hidden, down_full, preferred_element_type=jnp.float32)
    grad_mean = average_grads(slice_grads)
    return (branch.astype(jnp.bfloat16), grad_mean)


def solution(mesh):
    return jax.shard_map(
        per_device,
        mesh=mesh,
        in_specs=(
            P(("cuts", "fsdp"), None),
            P("fsdp"),
            P("fsdp", None),
            P("fsdp", None),
            P(None, "fsdp"),
            P("cuts", None, "fsdp", None),
        ),
        out_specs=(P(("cuts", "fsdp"), None), P(None, "fsdp", None)),
        check_vma=False,
    )
```

profile of v0, /device:TPU:0, one launch (start us, length us, event | category | flops | bytes accessed | tf_op | source)
XLA Modules:
  0.0 156.7 jit_solution(2685609127519770182)
XLA Ops:
  8.0 0.0 copy-start.1
  8.0 0.0 copy-start
  8.0 0.0 all-reduce.2.cloned.1.call-start
  8.1 0.7 all-reduce.2.cloned.1.call-update
  8.8 0.0 all-gather.4.cloned.1.call-start
  8.8 0.5 all-gather.4.cloned.1.call-update
  9.3 0.0 all-gather.6.cloned.1.call-start
  9.4 0.5 all-gather.6.cloned.1.call-update
  9.9 0.0 all-gather.8.cloned.1.call-start
  10.0 0.5 all-gather.8.cloned.1.call-update
  10.5 0.0 copy-done.1
  10.5 10.4 %all_gather.12 = bf16[8192]{0:T(1024)(128)(2,1)S(1)} all-gather(bf16[1024]{0:T(1024)(128)(2,1)S(1)} %copy-done.1), channel_id=1, replica_groups=mesh['cuts'=4,'fsdp'=8] {'fsdp'}, dimensions={0}, use_global_device_ids=true | all-gather | bytes 18432 | tf_op jit(solution)/shard_map/all_gather | solution.py:18
  20.9 0.0 copy-done
  20.9 0.5 fusion
  21.4 113.6 %all-reduce.2.cloned.1.call-done = f32[3,1024,256]{2,1,0:T(8,128)} async-done(((f32[3,1024,256]{2,1,0:T(8,128)}), f32[3,1024,256]{2,1,0:T(8,128)}) %all-reduce.2.cloned.1.call-update) | async-done | bytes 3145744 | tf_op jit(solution)/shard_map/psum | solution.py:8
  135.0 3.8 %broadcast_multiply_fusion = f32[3,1024,256]{2,1,0:T(8,128)} fusion(f32[3,1024,256]{2,1,0:T(8,128)} %all-reduce.2.cloned.1.call-done), kind=kLoop, calls=%fused_computation.6 | loop fusion | flops 786432 | bytes 6291456 | tf_op jit(solution)/shard_map/div | solution.py:9
  138.8 0.0 all-gather.4.cloned.1.call-done
  138.8 2.9 %fusion.6 = f32[128,256]{1,0:T(8,128)S(1)} fusion(bf16[8192,256]{1,0:T(8,128)(2,1)} %all-gather.4.cloned.1.call-done, bf16[128,8192]{1,0:T(8,128)(2,1)S(1)} %copy-done, f32[8192]{0:T(1024)S(1)} %convert_element_type.16, f32[128]{0:T(128)S(1)} %add_rsqrt_fusion), kind=kOutput, calls=%fused_computation.9 | convolution fusion | flops 541065216 | bytes 6455808 | tf_op jit(solution)/shard_map/dot_general | solution.py:21
  141.8 0.0 all-gather.6.cloned.1.call-done
  141.8 0.0 all-gather.8.cloned.1.call-done
  141.8 7.2 %convolution_convert_fusion = bf16[128,8192]{1,0:T(8,128)(2,1)} fusion(bf16[256,8192]{1,0:T(8,128)(2,1)} %all-gather.8.cloned.1.call-done, bf16[8192,256]{1,0:T(8,128)(2,1)} %all-gather.6.cloned.1.call-done, bf16[128,8192]{1,0:T(8,128)(2,1)S(1)} %copy-done, f32[8192]{0:T(1024)S(1)} %convert_element_type.16, f32[128]{0:T(128)S(1)} %add_rsqrt_fusion, ...), kind=kOutput, calls=%fused_computation | convolution fusion | flops 1079181312 | bytes 12747264 | tf_op jit(solution)/shard_map/dot_general | solution.py:25
  (2 shorter events, 0.0 us)
Async XLA Ops:
  8.0 2.5 %copy-start.1 = (bf16[1024]{0:T(1024)(128)(2,1)S(1)}, bf16[1024]{0:T(1024)(128)(2,1)}, u32[]{:S(2)}) copy-start(bf16[1024]{0:T(1024)(128)(2,1)} %param.7) | copy-start | bytes 6148
  8.0 12.9 %copy-start = (bf16[128,8192]{1,0:T(8,128)(2,1)S(1)}, bf16[128,8192]{1,0:T(8,128)(2,1)}, u32[]{:S(2)}) copy-start(bf16[128,8192]{1,0:T(8,128)(2,1)} %param.6) | copy-start | bytes 6291460
  8.0 127.0 %all-reduce.2.cloned.1.call-start = ((), (), s32[]{:S(2)}) async-start(), calls=%async_computation.3 | async-start | bytes 6291456 | tf_op jit(solution)/shard_map/psum | solution.py:8
  8.8 130.1 %all-gather.4.cloned.1.call-start = ((), (), s32[]{:S(2)}) async-start(), calls=%async_computation | async-start | bytes 4718592 | tf_op jit(solution)/shard_map/all_gather | solution.py:16
  9.3 132.5 %all-gather.6.cloned.1.call-start = ((), (), s32[]{:S(2)}) async-start(), calls=%async_computation.1 | async-start | bytes 4718592 | tf_op jit(solution)/shard_map/all_gather | solution.py:17
  9.9 131.9 %all-gather.8.cloned.1.call-start = ((), (), s32[]{:S(2)}) async-start(), calls=%async_computation.2 | async-start | bytes 4718592 | tf_op jit(solution)/shard_map/all_gather | solution.py:24
Sparse Core Ops, SparseCore 0:
  11.2 123.7 all-reduce.1
Sparse Core Ops, SparseCore 1:
  11.1 39.2 all-gather.3
  52.1 36.4 all-gather.5
  90.4 36.4 all-gather.7
where the time goes:
time: 157 us
  waiting for transfers between devices  116 us (74%)
  between operations  15.7 us (10%)
  blocking collectives  10.4 us (7%)
  matrix products  10.2 us (6%)
  other arithmetic  4.32 us (3%)
    psum x1, waiting for transfers between devices, average_grads(): summed = lax.psum(slice_grads[0], 'cuts')  114 us
    all_gather x1, blocking collectives, per_device(): lax.all_gather(norm_gain, 'fsdp', axis=0, tiled=True)  10.4 us
    dot_general x1, matrix products, per_device(): branch = jnp.dot(hidden, down_full, preferred_element_type=jnp.float32)  7.24 us
    div x1, other arithmetic, average_grads(): return summed / lax.axis_size('cuts')  3.82 us
  transfers between devices with their start and end apart: 4, of which 1 were waited for; matrix products, arithmetic and copies ran while one was open for 5% of the time, Pallas kernels for 0%

commit v1 on v0

--- a/solution.py
+++ b/solution.py
@@ -5,7 +5,7 @@
 
 
 def average_grads(slice_grads):
-    summed = lax.psum(slice_grads[0], "cuts")
+    summed = jnp.sum(lax.all_gather(slice_grads[0], "cuts"), axis=0)
     return summed / lax.axis_size("cuts")
 
 

time: 157 us -> 360 us (2.29)
  waiting for transfers between devices: 116 us -> 317 us
  other arithmetic: 4.32 us -> 8.25 us
    all_gather x0 -> x1, waiting for transfers between devices: none -> 212 us  [average_grads(): summed = jnp.sum(lax.all_gather(slice_grads[0], 'cuts'), axis=0)]
    psum x1 -> x0, waiting for transfers between devices: 114 us -> none  [average_grads(): summed = lax.psum(slice_grads[0], 'cuts')]
    all_gather x1, waiting for transfers between devices: 0.02 us -> 38.5 us  [per_device(): down_full = lax.all_gather(down_weight, 'fsdp', axis=1, tiled=True)]
    all_gather x1, waiting for transfers between devices: 0.03 us -> 35.6 us  [per_device(): lax.all_gather(up_weight, 'fsdp', axis=0, tiled=True)]
    all_gather x1, waiting for transfers between devices: 0.01 us -> 28.3 us  [per_device(): lax.all_gather(gate_weight, 'fsdp', axis=0, tiled=True)]
    reduce_sum x0 -> x1, other arithmetic: none -> 5.82 us  [average_grads(): summed = jnp.sum(lax.all_gather(slice_grads[0], 'cuts'), axis=0)]
  transfers between devices with their start and end apart: 4 -> 4, of which waited for: 1 -> 4; matrix products, arithmetic and copies ran while one was open for 5% -> 3% of each run, Pallas kernels for 0% -> 0%
where the time goes in v1:
time: 360 us
  waiting for transfers between devices  317 us (88%)
  between operations  13.8 us (4%)
  blocking collectives  10.4 us (3%)
  matrix products  10.2 us (3%)
  other arithmetic  8.25 us (2%)
    all_gather x1, waiting for transfers between devices, average_grads(): summed = jnp.sum(lax.all_gather(slice_grads[0], 'cuts'), axis=0)  212 us
    all_gather x1, waiting for transfers between devices, per_device(): down_full = lax.all_gather(down_weight, 'fsdp', axis=1, tiled=True)  38.5 us
    all_gather x1, waiting for transfers between devices, per_device(): lax.all_gather(up_weight, 'fsdp', axis=0, tiled=True)  35.6 us
    all_gather x1, waiting for transfers between devices, per_device(): lax.all_gather(gate_weight, 'fsdp', axis=0, tiled=True)  28.3 us
    all_gather x1, blocking collectives, per_device(): lax.all_gather(norm_gain, 'fsdp', axis=0, tiled=True)  10.4 us
    dot_general x1, matrix products, per_device(): branch = jnp.dot(hidden, down_full, preferred_element_type=jnp.float32)  7.23 us
  transfers between devices with their start and end apart: 4, of which 4 were waited for; matrix products, arithmetic and copies ran while one was open for 3% of the time, Pallas kernels for 0%

profile of v1, /device:TPU:0, one launch (start us, length us, event | category | flops | bytes accessed | tf_op | source)
XLA Modules:
  0.0 360.2 jit_solution(14441288608573569151)
XLA Ops:
  7.2 0.0 copy-start.1
  7.2 0.0 copy-start
  7.2 0.0 all-gather.5.cloned.1.call-start
  7.2 0.7 all-gather.5.cloned.1.call-update
  7.9 0.0 all-gather.7.cloned.1.call-start
  8.0 0.7 all-gather.7.cloned.1.call-update
  8.7 0.0 all-gather.9.cloned.1.call-start
  8.7 0.7 all-gather.9.cloned.1.call-update
  9.4 0.0 all-gather.11.cloned.1.call-start
  9.4 0.5 all-gather.11.cloned.1.call-update
  10.0 0.0 copy-done.1
  10.0 10.4 %all_gather.15 = bf16[8192]{0:T(1024)(128)(2,1)S(1)} all-gather(bf16[1024]{0:T(1024)(128)(2,1)S(1)} %copy-done.1), channel_id=1, replica_groups=mesh['cuts'=4,'fsdp'=8] {'fsdp'}, dimensions={0}, use_global_device_ids=true | all-gather | bytes 18432 | tf_op jit(solution)/shard_map/all_gather | solution.py:18
  20.4 0.0 copy-done
  20.4 0.5 fusion
  20.9 28.3 %all-gather.5.cloned.1.call-done = bf16[8192,256]{1,0:T(8,128)(2,1)} async-done(((bf16[1024,256]{1,0:T(8,128)(2,1)}), bf16[8192,256]{1,0:T(8,128)(2,1)}) %all-gather.5.cloned.1.call-update) | async-done | bytes 4194320 | tf_op jit(solution)/shard_map/all_gather | solution.py:16
  49.2 2.9 fusion.6
  52.2 35.6 %all-gather.7.cloned.1.call-done = bf16[8192,256]{1,0:T(8,128)(2,1)} async-done(((bf16[1024,256]{1,0:T(8,128)(2,1)}), bf16[8192,256]{1,0:T(8,128)(2,1)}) %all-gather.7.cloned.1.call-update) | async-done | bytes 4194320 | tf_op jit(solution)/shard_map/all_gather | solution.py:17
  87.7 38.5 %all-gather.9.cloned.1.call-done = bf16[256,8192]{1,0:T(8,128)(2,1)} async-done(((bf16[256,1024]{1,0:T(8,128)(2,1)}), bf16[256,8192]{1,0:T(8,128)(2,1)}) %all-gather.9.cloned.1.call-update) | async-done | bytes 4194320 | tf_op jit(solution)/shard_map/all_gather | solution.py:24
  126.2 7.2 %convolution_convert_fusion = bf16[128,8192]{1,0:T(8,128)(2,1)} fusion(bf16[256,8192]{1,0:T(8,128)(2,1)} %all-gather.9.cloned.1.call-done, bf16[8192,256]{1,0:T(8,128)(2,1)} %all-gather.7.cloned.1.call-done, bf16[128,8192]{1,0:T(8,128)(2,1)S(1)} %copy-done, f32[8192]{0:T(1024)S(1)} %convert_element_type.16, f32[128]{0:T(128)S(1)} %add_rsqrt_fusion, ...), kind=kOutput, calls=%fused_computation | convolution fusion | flops 1079181312 | bytes 12747264 | tf_op jit(solution)/shard_map/dot_general | solution.py:25
  133.5 212.4 %all-gather.11.cloned.1.call-done = f32[4,3,1024,256]{3,2,1,0:T(8,128)} async-done(((f32[1,3,1024,256]{3,2,1,0:T(8,128)}), f32[4,3,1024,256]{3,2,1,0:T(8,128)}) %all-gather.11.cloned.1.call-update) | async-done | bytes 12582928 | tf_op jit(solution)/shard_map/all_gather | solution.py:8
  345.9 5.8 %reduce_sum.19 = f32[3,1024,256]{2,1,0:T(8,128)S(1)} reduce(f32[4,3,1024,256]{3,2,1,0:T(8,128)} %all-gather.11.cloned.1.call-done, f32[]{:T(128)} %constant.3.clone.1), dimensions={0}, to_apply=%region_1.2 | reduce | flops 2359296 | bytes 15728644 | tf_op jit(solution)/shard_map/reduce_sum | solution.py:8
  351.7 1.9 broadcast_multiply_fusion
  (2 shorter events, 0.0 us)
Async XLA Ops:
  7.2 2.8 copy-start.1
  7.2 13.2 %copy-start = (bf16[128,8192]{1,0:T(8,128)(2,1)S(1)}, bf16[128,8192]{1,0:T(8,128)(2,1)}, u32[]{:S(2)}) copy-start(bf16[128,8192]{1,0:T(8,128)(2,1)} %param.6) | copy-start | bytes 6291460
  7.2 42.0 %all-gather.5.cloned.1.call-start = ((), (), s32[]{:S(2)}) async-start(), calls=%async_computation | async-start | bytes 4718592 | tf_op jit(solution)/shard_map/all_gather | solution.py:16
  7.9 79.8 %all-gather.7.cloned.1.call-start = ((), (), s32[]{:S(2)}) async-start(), calls=%async_computation.1 | async-start | bytes 4718592 | tf_op jit(solution)/shard_map/all_gather | solution.py:17
  8.7 117.6 %all-gather.9.cloned.1.call-start = ((), (), s32[]{:S(2)}) async-start(), calls=%async_computation.2 | async-start | bytes 4718592 | tf_op jit(solution)/shard_map/all_gather | solution.py:24
  9.4 336.5 %all-gather.11.cloned.1.call-start = ((), (), s32[]{:S(2)}) async-start(), calls=%async_computation.3 | async-start | bytes 15728640 | tf_op jit(solution)/shard_map/all_gather | solution.py:8
Sparse Core Ops, SparseCore 0:
  9.9 39.2 all-gather.4
  51.1 36.5 all-gather.6
  89.6 36.5 all-gather.8
  127.7 218.1 all-gather.10
